TPU v7x, 32 devices: a whole 2x2x4 slice. The times are simulated.
32 devices in a mesh: row: 8 (over z, y), col: 4 (over x, core).
Axes of the slice: x: 2, y: 2, z: 4, core: 2. Of those that a mesh axis runs over, the one named last changes fastest.
Arguments:
- matrix: bfloat16 [32768, 32768], P('row', 'col'), may hold values from -0.03125 to 0.03125
- right_sides: float32 [32768, 64], P(('row', 'col')), may hold values from -6 to 6
- initial_guess: float32 [32768, 64], P(('row', 'col')), may hold values from -6 to 6
Outputs:
- solution: float32 [32768, 64], P(('row', 'col'))
All inputs are finite; a program needn't handle non-finite values.
Results may differ from a plain program's by a relative error of at most 0.0038.
Values may be sent and summed in bfloat16 or wider, within the bound.
A program may use at most 128 MiB of HBM per device.

v0:
```python
import jax
import jax.numpy as jnp
from jax import lax
from jax.sharding import PartitionSpec as P

STEPS = 3
DIAGONAL_SHIFT = 1.4


def inner_products(left, right):
    return jnp.einsum("rk,rs->ks", left, right, precision=lax.Precision.HIGHEST)


def combine_basis(stacked, weights):
    return jnp.dot(stacked, weights, precision=lax.Precision.HIGHEST)


def orthonormal(applied, gram_sum):
    lower_factor = jnp.linalg.cholesky(gram_sum)
    basis_next = lax.linalg.triangular_solve(
        lower_factor, applied, left_side=False, lower=True, transpose_a=True
    )
    return (basis_next, lower_factor.T)


def least_squares(column_list, top_factor):
    span_width = top_factor.shape[0]
    count = len(column_list)
    pieces = []
    for position, (projected, upper_factor) in enumerate(column_list):
        filler = jnp.zeros(((count - position - 1) * span_width, span_width), jnp.float32)
        pieces.append(jnp.concatenate([projected, upper_factor, filler], axis=0))
    hessenberg = jnp.concatenate(pieces, axis=1)
    normal_matrix = inner_products(hessenberg, hessenberg)
    target = inner_products(hessenberg[:span_width], top_factor)
    lower_factor = jnp.linalg.cholesky(normal_matrix)
    halfway = lax.linalg.triangular_solve(lower_factor, target, left_side=True, lower=True)
    return lax.linalg.triangular_solve(
        lower_factor, halfway, left_side=True, lower=True, transpose_a=True
    )


def per_device(matrix, right_sides, initial_guess):

    def fold_panel(panel_piece):
        return jnp.dot(matrix, panel_piece, preferred_element_type=jnp.float32)

    def operate(local_block):
        operand = local_block.astype(jnp.bfloat16)
        partial_sum = fold_panel(lax.all_gather(operand, "row", axis=0, tiled=True))
        product = lax.psum_scatter(partial_sum, "col", scatter_dimension=0, tiled=True)
        return DIAGONAL_SHIFT * local_block + product

    def reduce_all(local_sum):
        return lax.psum(local_sum, ("row", "col"))

    guess_local, sides_local = (initial_guess, right_sides)
    residual_start = sides_local - operate(guess_local)
    basis_now, top_factor = orthonormal(
        residual_start, reduce_all(inner_products(residual_start, residual_start))
    )
    basis_list = [basis_now]
    column_list = []
    for iteration in range(STEPS):
        applied = operate(basis_list[-1])
        stacked = jnp.concatenate(basis_list, axis=1)
        span_width = stacked.shape[1]
        combined = reduce_all(inner_products(jnp.concatenate([stacked, applied], axis=1), applied))
        projected = combined[:span_width]
        gram_sum = combined[span_width:] - inner_products(projected, projected)
        applied = applied - combine_basis(stacked, projected)
        basis_now, upper_factor = orthonormal(applied, gram_sum)
        basis_list.append(basis_now)
        column_list.append((projected, upper_factor))
    coefficients = least_squares(column_list, top_factor)
    update = combine_basis(jnp.concatenate(basis_list[:-1], axis=1), coefficients)
    return guess_local + update


def solution(mesh):
    return jax.shard_map(
        per_device,
        mesh=mesh,
        in_specs=(P("row", "col"), P(("row", "col"), None), P(("row", "col"), None)),
        out_specs=P(("row", "col"), None),
        check_vma=False,
    )
```

profile of v0, /device:TPU:1, one launch (start us, length us, event | category | flops | bytes accessed | tf_op | source)
XLA Modules:
  0.0 751.0 jit_solution(7809911143641430685)
XLA Ops:
  6.5 1.7 convert_element_type.12
  8.3 41.9 %all-gather.5.cloned.1.call-done = bf16[8192,64]{0,1:T(8,128)(2,1)} async-done(((bf16[1024,64]{0,1:T(8,128)(2,1)}), bf16[8192,64]{0,1:T(8,128)(2,1)}) %all-gather.5.cloned.1.call-update) | async-done | bytes 1048592 | tf_op jit(solution)/shard_map/all_gather | solution.py:50
  50.2 29.6 %fusion.97 = f32[4096,64]{0,1:T(8,128)} fusion(bf16[4096,8192]{1,0:T(8,128)(2,1)} %param.6, bf16[8192,64]{0,1:T(8,128)(2,1)} %all-gather.5.cloned.1.call-done), kind=kOutput, calls=%fused_computation.157 | convolution fusion | flops 4294967296 | bytes 69206016 | tf_op jit(solution)/shard_map/dot_general | solution.py:46
  79.9 25.2 %reduce-scatter.5.cloned.1.call-done = f32[1024,64]{0,1:T(8,128)} async-done(((f32[4096,64]{0,1:T(8,128)}), f32[1024,64]{0,1:T(8,128)}) %reduce-scatter.5.cloned.1.call-update) | async-done | bytes 262160 | tf_op jit(solution)/shard_map/reduce_scatter | solution.py:51
  105.0 1.4 fusion.93
  106.5 38.8 %psum.28 = f32[64,64]{0,1:T(8,128)S(1)} all-reduce(f32[64,64]{0,1:T(8,128)S(1)} %fusion.93), channel_id=1, replica_groups=mesh['row'=8,'col'=4] {'row','col'}, use_global_device_ids=true, to_apply=%region_1.0 | all-reduce | flops 4096 | bytes 32768 | tf_op jit(solution)/shard_map/psum | solution.py:55
  145.4 5.8 cholesky.195
  152.6 4.9 custom-call.25
  157.5 2.0 fusion.94
  159.6 40.1 %all-gather.7.cloned.1.call-done = bf16[8192,64]{0,1:T(8,128)(2,1)} async-done(((bf16[1024,64]{0,1:T(8,128)(2,1)}), bf16[8192,64]{0,1:T(8,128)(2,1)}) %all-gather.7.cloned.1.call-update) | async-done | bytes 1048592 | tf_op jit(solution)/shard_map/all_gather | solution.py:50
  199.7 28.4 %convolution_bitcast_fusion.2 = f32[4096,64]{0,1:T(8,128)} fusion(bf16[8192,64]{0,1:T(8,128)(2,1)} %all-gather.7.cloned.1.call-done, bf16[4096,8192]{1,0:T(8,128)(2,1)} %param.6), kind=kOutput, calls=%fused_computation.2 | convolution fusion | flops 4294967296 | bytes 69206016 | tf_op jit(solution)/shard_map/dot_general | solution.py:46
  228.2 25.1 %reduce-scatter.7.cloned.1.call-done = f32[1024,64]{0,1:T(8,128)} async-done(((f32[4096,64]{0,1:T(8,128)}), f32[1024,64]{0,1:T(8,128)}) %reduce-scatter.7.cloned.1.call-update) | async-done | bytes 262160 | tf_op jit(solution)/shard_map/reduce_scatter | solution.py:51
  255.0 39.0 %psum.29 = f32[128,64]{0,1:T(8,128)S(1)} all-reduce(f32[128,64]{0,1:T(8,128)S(1)} %fusion.13), channel_id=1, replica_groups=mesh['row'=8,'col'=4] {'row','col'}, use_global_device_ids=true, to_apply=%region_5.8 | all-reduce | flops 8192 | bytes 65536 | tf_op jit(solution)/shard_map/psum | solution.py:55
  294.3 5.8 cholesky.206
  301.5 4.9 custom-call.26
  308.9 40.2 %all-gather.9.cloned.1.call-done = bf16[8192,64]{0,1:T(8,128)(2,1)} async-done(((bf16[1024,64]{0,1:T(8,128)(2,1)}), bf16[8192,64]{0,1:T(8,128)(2,1)}) %all-gather.9.cloned.1.call-update) | async-done | bytes 1048592 | tf_op jit(solution)/shard_map/all_gather | solution.py:50
  349.1 28.4 %convolution_bitcast_fusion.1 = f32[4096,64]{0,1:T(8,128)} fusion(bf16[8192,64]{0,1:T(8,128)(2,1)} %all-gather.9.cloned.1.call-done, bf16[4096,8192]{1,0:T(8,128)(2,1)} %param.6), kind=kOutput, calls=%fused_computation.1 | convolution fusion | flops 4294967296 | bytes 69206016 | tf_op jit(solution)/shard_map/dot_general | solution.py:46
  377.6 25.2 %reduce-scatter.9.cloned.1.call-done = f32[1024,64]{0,1:T(8,128)} async-done(((f32[4096,64]{0,1:T(8,128)}), f32[1024,64]{0,1:T(8,128)}) %reduce-scatter.9.cloned.1.call-update) | async-done | bytes 262160 | tf_op jit(solution)/shard_map/reduce_scatter | solution.py:51
  404.6 39.0 %psum.30 = f32[192,64]{0,1:T(8,128)S(1)} all-reduce(f32[192,64]{0,1:T(8,128)S(1)} %fusion.8), channel_id=1, replica_groups=mesh['row'=8,'col'=4] {'row','col'}, use_global_device_ids=true, to_apply=%region_7.10 | all-reduce | flops 12288 | bytes 98304 | tf_op jit(solution)/shard_map/psum | solution.py:55
  443.8 5.8 cholesky.217
  451.0 4.9 custom-call.27
  458.5 40.2 %all-gather.11.cloned.1.call-done = bf16[8192,64]{0,1:T(8,128)(2,1)} async-done(((bf16[1024,64]{0,1:T(8,128)(2,1)}), bf16[8192,64]{0,1:T(8,128)(2,1)}) %all-gather.11.cloned.1.call-update) | async-done | bytes 1048592 | tf_op jit(solution)/shard_map/all_gather | solution.py:50
  498.7 28.4 %convolution_bitcast_fusion = f32[4096,64]{0,1:T(8,128)} fusion(bf16[8192,64]{0,1:T(8,128)(2,1)} %all-gather.11.cloned.1.call-done, bf16[4096,8192]{1,0:T(8,128)(2,1)} %param.6), kind=kOutput, calls=%fused_computation | convolution fusion | flops 4294967296 | bytes 69206016 | tf_op jit(solution)/shard_map/dot_general | solution.py:46
  527.4 24.9 %reduce-scatter.11.cloned.1.call-done = f32[1024,64]{0,1:T(8,128)} async-done(((f32[4096,64]{0,1:T(8,128)}), f32[1024,64]{0,1:T(8,128)}) %reduce-scatter.11.cloned.1.call-update) | async-done | bytes 262160 | tf_op jit(solution)/shard_map/reduce_scatter | solution.py:51
  553.3 1.7 fusion
  555.1 124.3 %all-reduce.5.cloned.1.call-done = f32[256,64]{0,1:T(8,128)} async-done(((f32[256,64]{0,1:T(8,128)}), f32[256,64]{0,1:T(8,128)}) %all-reduce.5.cloned.1.call-update) | async-done | bytes 65552 | tf_op jit(solution)/shard_map/psum | solution.py:55
  680.6 5.8 cholesky.228
  689.3 11.7 %cholesky.77 = f32[128,128]{1,0:T(8,128)S(1)} custom-call(f32[128,128]{1,0:T(8,128)S(1)} %cholesky.237), custom_call_target="Cholesky" | custom-call | tf_op jit(solution)/shard_map/jit(cholesky)/cholesky | solution.py:36
  701.1 1.8 fusion.33
  702.9 9.8 %custom-call.21 = f32[1,128,128]{1,2,0:T(8,128)S(1)} custom-call(f32[1,128,128]{2,1,0:T(8,128)S(1)} %get-tuple-element.28), custom_call_target="InvertDiagBlocksLowerTriangular" | custom-call | tf_op jit(solution)/shard_map/jit(cholesky)/cholesky | solution.py:36
  713.1 5.8 cholesky.135
  721.8 19.9 %custom-call.22 = f32[2,128,128]{1,2,0:T(8,128)S(1)} custom-call(f32[2,128,128]{2,1,0:T(8,128)S(1)} %pad_maximum_fusion.7), custom_call_target="InvertDiagBlocksLowerTriangular" | custom-call | tf_op jit(solution)/shard_map/triangular_solve | solution.py:38
  (82 shorter events, 23.3 us)
Async XLA Ops:
  6.5 98.5 %copy-start = (f32[1024,64]{0,1:T(8,128)S(1)}, f32[1024,64]{0,1:T(8,128)}, u32[]{:S(2)}) copy-start(f32[1024,64]{0,1:T(8,128)} %param.8) | copy-start | bytes 786436
  6.5 98.5 %copy-start.1 = (f32[1024,64]{0,1:T(8,128)S(1)}, f32[1024,64]{0,1:T(8,128)}, u32[]{:S(2)}) copy-start(f32[1024,64]{0,1:T(8,128)} %param.7) | copy-start | bytes 786436
  6.5 43.6 %all-gather.5.cloned.1.call-start = ((), (), s32[]{:S(2)}) async-start(), calls=%async_computation.4 | async-start | bytes 1179648 | tf_op jit(solution)/shard_map/all_gather | solution.py:50
  8.3 96.8 %reduce-scatter.5.cloned.1.call-start = ((), (), s32[]{:S(2)}) async-start(), calls=%async_computation.5 | async-start | bytes 1310720 | tf_op jit(solution)/shard_map/reduce_scatter | solution.py:51
  79.8 119.9 %all-gather.7.cloned.1.call-start = ((), (), s32[]{:S(2)}) async-start(), calls=%async_computation.6 | async-start | bytes 1179648 | tf_op jit(solution)/shard_map/all_gather | solution.py:50
  159.6 93.8 %reduce-scatter.7.cloned.1.call-start = ((), (), s32[]{:S(2)}) async-start(), calls=%async_computation.7 | async-start | bytes 1310720 | tf_op jit(solution)/shard_map/reduce_scatter | solution.py:51
  228.2 121.0 %all-gather.9.cloned.1.call-start = ((), (), s32[]{:S(2)}) async-start(), calls=%async_computation.8 | async-start | bytes 1179648 | tf_op jit(solution)/shard_map/all_gather | solution.py:50
  308.9 93.9 %reduce-scatter.9.cloned.1.call-start = ((), (), s32[]{:S(2)}) async-start(), calls=%async_computation.9 | async-start | bytes 1310720 | tf_op jit(solution)/shard_map/reduce_scatter | solution.py:51
  377.5 121.2 %all-gather.11.cloned.1.call-start = ((), (), s32[]{:S(2)}) async-start(), calls=%async_computation.10 | async-start | bytes 1179648 | tf_op jit(solution)/shard_map/all_gather | solution.py:50
  458.4 93.9 %reduce-scatter.11.cloned.1.call-start = ((), (), s32[]{:S(2)}) async-start(), calls=%async_computation.11 | async-start | bytes 1310720 | tf_op jit(solution)/shard_map/reduce_scatter | solution.py:51
  527.1 152.3 %all-reduce.5.cloned.1.call-start = ((), (), s32[]{:S(2)}) async-start(), calls=%async_computation.12 | async-start | bytes 131072 | tf_op jit(solution)/shard_map/psum | solution.py:55
Sparse Core Ops, SparseCore 0:
  9.5 40.6 all-gather.4
  79.9 25.0 reduce-scatter.4
  159.7 40.0 all-gather.6
  228.3 25.0 reduce-scatter.6
  309.0 40.0 all-gather.8
  377.6 25.0 reduce-scatter.8
  458.5 40.1 all-gather.10
  527.2 25.0 reduce-scatter.10
  557.9 121.4 all-reduce.4
where the time goes:
time: 752 us; the launch traced here: 751 us
  waiting for transfers between devices  387 us (51%)
  matrix products  134 us (18%)
  blocking collectives  117 us (16%)
  other arithmetic  96.9 us (13%)
  between operations  14.9 us (2%)
    all_gather x4, waiting for transfers between devices, operate(): partial_sum = fold_panel(lax.all_gather(operand, 'row', axis=0, tiled=True))  162 us
    psum x1, waiting for transfers between devices, reduce_all(): return lax.psum(local_sum, ('row', 'col'))  124 us
    psum x3, blocking collectives, reduce_all(): return lax.psum(local_sum, ('row', 'col'))  117 us
    dot_general x4, matrix products, fold_panel(): return jnp.dot(matrix, panel_piece, preferred_element_type=jnp.float32)  115 us
    reduce_scatter x4, waiting for transfers between devices, operate(): lax.psum_scatter(partial_sum, 'col', scatter_dimension=0, tiled=True)  100 us
    another operation x7, other arithmetic, least_squares(): lower_factor = jnp.linalg.cholesky(normal_matrix)  28.8 us
    another operation x12, other arithmetic, orthonormal(): lower_factor = jnp.linalg.cholesky(gram_sum)  26.1 us
    another operation x6, other arithmetic, least_squares(): lax.linalg.triangular_solve(lower_factor, halfway, left_side=True, lower=...  20.1 us
  transfers between devices with their start and end apart: 9, of which 9 were waited for; matrix products, arithmetic and copies ran while one was open for 0% of the time, Pallas kernels for 0%

commit v1 on v0

--- a/solution.py
+++ b/solution.py
@@ -52,7 +52,7 @@
         return DIAGONAL_SHIFT * local_block + product
 
     def reduce_all(local_sum):
-        return lax.psum(local_sum, ("row", "col"))
+        return jnp.sum(lax.all_gather(local_sum, ("row", "col")), axis=0)
 
     guess_local, sides_local = (initial_guess, right_sides)
     residual_start = sides_local - operate(guess_local)

time: 752 us -> 714 us (0.949)
  blocking collectives: 117 us -> 44.2 us
  waiting for transfers between devices: 387 us -> 418 us
    all_gather x0 -> x3, waiting for transfers between devices: none -> 166 us  [reduce_all(): return jnp.sum(lax.all_gather(local_sum, ('row', 'col')), axis=0)]
    psum x1 -> x0, waiting for transfers between devices: 124 us -> none  [reduce_all(): return lax.psum(local_sum, ('row', 'col'))]
    psum x3 -> x0, blocking collectives: 117 us -> none  [reduce_all(): return lax.psum(local_sum, ('row', 'col'))]
    all_gather x0 -> x1, blocking collectives: none -> 44.2 us  [reduce_all(): return jnp.sum(lax.all_gather(local_sum, ('row', 'col')), axis=0)]
    all_gather x4, waiting for transfers between devices: 162 us -> 151 us  [operate(): partial_sum = fold_panel(lax.all_gather(operand, 'row', axis=0, tiled=True))]
  transfers between devices with their start and end apart: 9 -> 11, of which waited for: 9 -> 11; matrix products, arithmetic and copies ran while one was open for 0% -> 0% of each run, Pallas kernels for 0% -> 0%
where the time goes in v1:
time: 714 us; the launch traced here: 713 us
  waiting for transfers between devices  418 us (59%)
  matrix products  132 us (18%)
  other arithmetic  99 us (14%)
  blocking collectives  44.2 us (6%)
  between operations  14.9 us (2%)
    all_gather x3, waiting for transfers between devices, reduce_all(): return jnp.sum(lax.all_gather(local_sum, ('row', 'col')), axis=0)  166 us
    all_gather x4, waiting for transfers between devices, operate(): partial_sum = fold_panel(lax.all_gather(operand, 'row', axis=0, tiled=True))  151 us
    dot_general x4, matrix products, fold_panel(): return jnp.dot(matrix, panel_piece, preferred_element_type=jnp.float32)  115 us
    reduce_scatter x4, waiting for transfers between devices, operate(): lax.psum_scatter(partial_sum, 'col', scatter_dimension=0, tiled=True)  100 us
    all_gather x1, blocking collectives, reduce_all(): return jnp.sum(lax.all_gather(local_sum, ('row', 'col')), axis=0)  44.2 us
    another operation x7, other arithmetic, least_squares(): lower_factor = jnp.linalg.cholesky(normal_matrix)  28.8 us
    another operation x12, other arithmetic, orthonormal(): lower_factor = jnp.linalg.cholesky(gram_sum)  26.1 us
    another operation x6, other arithmetic, least_squares(): lax.linalg.triangular_solve(lower_factor, halfway, left_side=True, lower=...  20.1 us
  transfers between devices with their start and end apart: 11, of which 11 were waited for; matrix products, arithmetic and copies ran while one was open for 0% of the time, Pallas kernels for 0%

profile of v1, /device:TPU:1, one launch (start us, length us, event | category | flops | bytes accessed | tf_op | source)
XLA Modules:
  0.0 713.1 jit_solution(17694571819994403369)
XLA Ops:
  6.5 1.7 convert_element_type.12
  8.3 41.9 %all-gather.13.cloned.1.call-done = bf16[8192,64]{0,1:T(8,128)(2,1)} async-done(((bf16[1024,64]{0,1:T(8,128)(2,1)}), bf16[8192,64]{0,1:T(8,128)(2,1)}) %all-gather.13.cloned.1.call-update) | async-done | bytes 1048592 | tf_op jit(solution)/shard_map/all_gather | solution.py:50
  50.2 29.6 %fusion.96 = f32[4096,64]{0,1:T(8,128)} fusion(bf16[4096,8192]{1,0:T(8,128)(2,1)} %param.6, bf16[8192,64]{0,1:T(8,128)(2,1)} %all-gather.13.cloned.1.call-done), kind=kOutput, calls=%fused_computation.159 | convolution fusion | flops 4294967296 | bytes 69206016 | tf_op jit(solution)/shard_map/dot_general | solution.py:46
  79.9 25.2 %reduce-scatter.5.cloned.1.call-done = f32[1024,64]{0,1:T(8,128)} async-done(((f32[4096,64]{0,1:T(8,128)}), f32[1024,64]{0,1:T(8,128)}) %reduce-scatter.5.cloned.1.call-update) | async-done | bytes 262160 | tf_op jit(solution)/shard_map/reduce_scatter | solution.py:51
  106.5 44.2 %all-gather = f32[2048,64]{1,0:T(8,128)S(1)} all-gather(f32[64,64]{1,0:T(8,128)S(1)} %fusion.92), channel_id=2, replica_groups=mesh['row'=8,'col'=4] {'row','col'}, dimensions={0}, use_global_device_ids=true | all-gather | bytes 540672 | tf_op jit(solution)/shard_map/all_gather | solution.py:55
  150.8 5.8 cholesky.195
  157.9 4.9 custom-call.25
  162.8 2.0 fusion.93
  165.0 34.3 %all-gather.15.cloned.1.call-done = bf16[8192,64]{0,1:T(8,128)(2,1)} async-done(((bf16[1024,64]{0,1:T(8,128)(2,1)}), bf16[8192,64]{0,1:T(8,128)(2,1)}) %all-gather.15.cloned.1.call-update) | async-done | bytes 1048592 | tf_op jit(solution)/shard_map/all_gather | solution.py:50
  199.2 28.4 %convolution_bitcast_fusion.2 = f32[4096,64]{0,1:T(8,128)} fusion(bf16[8192,64]{0,1:T(8,128)(2,1)} %all-gather.15.cloned.1.call-done, bf16[4096,8192]{1,0:T(8,128)(2,1)} %param.6), kind=kOutput, calls=%fused_computation.2 | convolution fusion | flops 4294967296 | bytes 69206016 | tf_op jit(solution)/shard_map/dot_general | solution.py:46
  227.7 25.2 %reduce-scatter.7.cloned.1.call-done = f32[1024,64]{0,1:T(8,128)} async-done(((f32[4096,64]{0,1:T(8,128)}), f32[1024,64]{0,1:T(8,128)}) %reduce-scatter.7.cloned.1.call-update) | async-done | bytes 262160 | tf_op jit(solution)/shard_map/reduce_scatter | solution.py:51
  255.2 53.3 %all-gather.21.cloned.1.call-done = f32[4096,64]{0,1:T(8,128)} async-done(((f32[128,64]{0,1:T(8,128)}), f32[4096,64]{0,1:T(8,128)}) %all-gather.21.cloned.1.call-update) | async-done | bytes 1048592 | tf_op jit(solution)/shard_map/all_gather | solution.py:55
  310.3 5.8 cholesky.206
  317.4 4.9 custom-call.26
  325.0 37.8 %all-gather.17.cloned.1.call-done = bf16[8192,64]{0,1:T(8,128)(2,1)} async-done(((bf16[1024,64]{0,1:T(8,128)(2,1)}), bf16[8192,64]{0,1:T(8,128)(2,1)}) %all-gather.17.cloned.1.call-update) | async-done | bytes 1048592 | tf_op jit(solution)/shard_map/all_gather | solution.py:50
  362.8 28.4 %convolution_bitcast_fusion.1 = f32[4096,64]{0,1:T(8,128)} fusion(bf16[8192,64]{0,1:T(8,128)(2,1)} %all-gather.17.cloned.1.call-done, bf16[4096,8192]{1,0:T(8,128)(2,1)} %param.6), kind=kOutput, calls=%fused_computation.1 | convolution fusion | flops 4294967296 | bytes 69206016 | tf_op jit(solution)/shard_map/dot_general | solution.py:46
  391.2 25.1 %reduce-scatter.9.cloned.1.call-done = f32[1024,64]{0,1:T(8,128)} async-done(((f32[4096,64]{0,1:T(8,128)}), f32[1024,64]{0,1:T(8,128)}) %reduce-scatter.9.cloned.1.call-update) | async-done | bytes 262160 | tf_op jit(solution)/shard_map/reduce_scatter | solution.py:51
  419.0 57.1 %all-gather.25.cloned.1.call-done = f32[32,192,64]{1,2,0:T(8,128)} async-done(((f32[1,192,64]{1,2,0:T(8,128)}), f32[32,192,64]{1,2,0:T(8,128)}) %all-gather.25.cloned.1.call-update) | async-done | bytes 1572880 | tf_op jit(solution)/shard_map/all_gather | solution.py:55
  476.0 1.7 reduce_sum.38
  478.0 5.8 cholesky.217
  485.2 4.9 custom-call.27
  492.7 37.1 %all-gather.19.cloned.1.call-done = bf16[8192,64]{0,1:T(8,128)(2,1)} async-done(((bf16[1024,64]{0,1:T(8,128)(2,1)}), bf16[8192,64]{0,1:T(8,128)(2,1)}) %all-gather.19.cloned.1.call-update) | async-done | bytes 1048592 | tf_op jit(solution)/shard_map/all_gather | solution.py:50
  529.8 28.4 %convolution_bitcast_fusion = f32[4096,64]{0,1:T(8,128)} fusion(bf16[8192,64]{0,1:T(8,128)(2,1)} %all-gather.19.cloned.1.call-done, bf16[4096,8192]{1,0:T(8,128)(2,1)} %param.6), kind=kOutput, calls=%fused_computation | convolution fusion | flops 4294967296 | bytes 69206016 | tf_op jit(solution)/shard_map/dot_general | solution.py:46
  558.5 24.9 %reduce-scatter.11.cloned.1.call-done = f32[1024,64]{0,1:T(8,128)} async-done(((f32[4096,64]{0,1:T(8,128)}), f32[1024,64]{0,1:T(8,128)}) %reduce-scatter.11.cloned.1.call-update) | async-done | bytes 262160 | tf_op jit(solution)/shard_map/reduce_scatter | solution.py:51
  584.4 1.7 fusion
  586.2 55.6 %all-gather.23.cloned.1.call-done = f32[8192,64]{0,1:T(8,128)} async-done(((f32[256,64]{0,1:T(8,128)}), f32[8192,64]{0,1:T(8,128)}) %all-gather.23.cloned.1.call-update) | async-done | bytes 2097168 | tf_op jit(solution)/shard_map/all_gather | solution.py:55
  641.7 2.2 copy.40
  644.5 5.8 cholesky.228
  653.2 11.7 %cholesky.77 = f32[128,128]{1,0:T(8,128)S(1)} custom-call(f32[128,128]{1,0:T(8,128)S(1)} %cholesky.237), custom_call_target="Cholesky" | custom-call | tf_op jit(solution)/shard_map/jit(cholesky)/cholesky | solution.py:36
  665.0 9.8 %custom-call.21 = f32[1,128,128]{1,2,0:T(8,128)S(1)} custom-call(f32[1,128,128]{2,1,0:T(8,128)S(1)} %get-tuple-element.28), custom_call_target="InvertDiagBlocksLowerTriangular" | custom-call | tf_op jit(solution)/shard_map/jit(cholesky)/cholesky | solution.py:36
  675.2 5.8 cholesky.135
  683.9 19.9 %custom-call.22 = f32[2,128,128]{1,2,0:T(8,128)S(1)} custom-call(f32[2,128,128]{2,1,0:T(8,128)S(1)} %pad_maximum_fusion.7), custom_call_target="InvertDiagBlocksLowerTriangular" | custom-call | tf_op jit(solution)/shard_map/triangular_solve | solution.py:38
  (92 shorter events, 27.1 us)
Async XLA Ops:
  6.5 98.5 %copy-start = (f32[1024,64]{0,1:T(8,128)S(1)}, f32[1024,64]{0,1:T(8,128)}, u32[]{:S(2)}) copy-start(f32[1024,64]{0,1:T(8,128)} %param.8) | copy-start | bytes 786436
  6.5 98.5 %copy-start.1 = (f32[1024,64]{0,1:T(8,128)S(1)}, f32[1024,64]{0,1:T(8,128)}, u32[]{:S(2)}) copy-start(f32[1024,64]{0,1:T(8,128)} %param.7) | copy-start | bytes 786436
  6.5 43.6 %all-gather.13.cloned.1.call-start = ((), (), s32[]{:S(2)}) async-start(), calls=%async_computation.4 | async-start | bytes 1179648 | tf_op jit(solution)/shard_map/all_gather | solution.py:50
  8.3 96.8 %reduce-scatter.5.cloned.1.call-start = ((), (), s32[]{:S(2)}) async-start(), calls=%async_computation.5 | async-start | bytes 1310720 | tf_op jit(solution)/shard_map/reduce_scatter | solution.py:51
  79.8 119.4 %all-gather.15.cloned.1.call-start = ((), (), s32[]{:S(2)}) async-start(), calls=%async_computation.6 | async-start | bytes 1179648 | tf_op jit(solution)/shard_map/all_gather | solution.py:50
  164.9 87.9 %reduce-scatter.7.cloned.1.call-start = ((), (), s32[]{:S(2)}) async-start(), calls=%async_computation.7 | async-start | bytes 1310720 | tf_op jit(solution)/shard_map/reduce_scatter | solution.py:51
  227.6 80.8 %all-gather.21.cloned.1.call-start = ((), (), s32[]{:S(2)}) async-start(), calls=%async_computation.12 | async-start | bytes 1081344 | tf_op jit(solution)/shard_map/all_gather | solution.py:55
  255.1 107.6 %all-gather.17.cloned.1.call-start = ((), (), s32[]{:S(2)}) async-start(), calls=%async_computation.8 | async-start | bytes 1179648 | tf_op jit(solution)/shard_map/all_gather | solution.py:50
  324.8 91.6 %reduce-scatter.9.cloned.1.call-start = ((), (), s32[]{:S(2)}) async-start(), calls=%async_computation.9 | async-start | bytes 1310720 | tf_op jit(solution)/shard_map/reduce_scatter | solution.py:51
  391.2 84.8 %all-gather.25.cloned.1.call-start = ((), (), s32[]{:S(2)}) async-start(), calls=%async_computation.14 | async-start | bytes 2162688 | tf_op jit(solution)/shard_map/all_gather | solution.py:55
  418.9 110.9 %all-gather.19.cloned.1.call-start = ((), (), s32[]{:S(2)}) async-start(), calls=%async_computation.10 | async-start | bytes 1179648 | tf_op jit(solution)/shard_map/all_gather | solution.py:50
  492.6 90.8 %reduce-scatter.11.cloned.1.call-start = ((), (), s32[]{:S(2)}) async-start(), calls=%async_computation.11 | async-start | bytes 1310720 | tf_op jit(solution)/shard_map/reduce_scatter | solution.py:51
  558.2 83.5 %all-gather.23.cloned.1.call-start = ((), (), s32[]{:S(2)}) async-start(), calls=%async_computation.13 | async-start | bytes 2162688 | tf_op jit(solution)/shard_map/all_gather | solution.py:55
Sparse Core Ops, SparseCore 0:
  9.5 40.6 all-gather.12
  79.9 25.0 reduce-scatter.4
  165.0 34.1 all-gather.14
  227.7 25.0 reduce-scatter.6
  255.6 52.8 all-gather.20
  324.9 37.8 all-gather.16
  391.3 25.0 reduce-scatter.8
  419.2 56.7 all-gather.24
  492.7 37.0 all-gather.18
  558.3 25.0 reduce-scatter.10
  586.3 55.3 all-gather.22
